TPU v7x, 32 devices: a whole 2x2x4 slice. The times are simulated.
32 devices in a mesh: groups: 1, slab: 8 (over z, y), coil: 2 (over x), row: 2 (over core).
Axes of the slice: x: 2, y: 2, z: 4, core: 2. Of those that a mesh axis runs over, the one named last changes fastest.
Arguments:
- image: float32 [2, 128, 256, 128], P('groups', None, ('slab', 'row')), may hold values from -6 to 6
- sens: bfloat16 [2, 16, 128, 256, 128], P('groups', 'coil', None, ('slab', 'row')), may hold values from -1.5 to 1.5
- measured: bfloat16 [2, 16, 128, 256, 128], P('groups', 'coil', ('slab', 'row')), may hold values from -3 to 3
- mask: int32 [128, 256], P(('slab', 'row')), may hold values from 0 to 1, as said below
- thresholds: float32 [2, 7], replicated, may hold values from 0.1 to 1.5
Outputs:
- image_next: float32 [2, 128, 256, 128], P('groups', None, ('slab', 'row'))
Inputs may be any that keep to these rules, and one draw needn't show every extreme that they name: `mask`: A calibration block of the 8 central phase-encode lines (ky from 60 to 67) is sampled at every kz; outside it each (ky, kz) is sampled independently at random.
All inputs are finite; a program needn't handle non-finite values.
Results may differ from a plain program's by a relative error of at most 0.013.
Values may be sent and summed in bfloat16 or wider, within the bound.
A program may use at most 128 MiB of HBM per device.

v0:
```python
import math
import jax
import jax.numpy as jnp
from jax import lax
from jax.sharding import PartitionSpec as P

half_root = 0.7071067811865476
quarter_root = 0.3535533905932738
step_size = 0.5


def passed_along(block, axis, distance):
    devices = range(lax.axis_size(axis))
    route = [((i - distance) % len(devices), i) for i in devices]
    return lax.ppermute(block, axis, route)


def fourier_table(length, sign):
    index = jnp.arange(length, dtype=jnp.int32)
    phase = index[:, None] * index[None, :] % length
    theta = phase.astype(jnp.float32) * jnp.float32(2.0 * math.pi / length)
    scale = jnp.float32(1.0 / math.sqrt(length))
    real = jnp.cos(theta) * scale
    imaginary = jnp.sin(theta) * (sign * scale)
    upper = jnp.stack([real, -imaginary])
    lower = jnp.stack([imaginary, real])
    return jnp.stack([upper, lower]).astype(jnp.bfloat16)


def contract(form, values, table):
    return jnp.einsum(form, values, table, preferred_element_type=jnp.float32)


def complex_product(left, right):
    return jnp.stack(
        [left[0] * right[0] - left[1] * right[1], left[0] * right[1] + left[1] * right[0]]
    )


def roll_after(values, along, offset):
    return jnp.roll(values, -offset, axis=along)


def roll_before(values, along, offset):
    return jnp.roll(values, offset, axis=along)


def plane_after(values, along, offset):
    border = lax.slice_in_dim(values, 0, offset, axis=along)
    fetched = passed_along(border.astype(jnp.bfloat16), ("slab", "row"), -1).astype(border.dtype)
    remain = lax.slice_in_dim(values, offset, values.shape[along], axis=along)
    return jnp.concatenate([remain, fetched], axis=along)


def plane_before(values, along, offset):
    extent = values.shape[along]
    border = lax.slice_in_dim(values, extent - offset, extent, axis=along)
    fetched = passed_along(border.astype(jnp.bfloat16), ("slab", "row"), 1).astype(border.dtype)
    remain = lax.slice_in_dim(values, 0, extent - offset, axis=along)
    return jnp.concatenate([fetched, remain], axis=along)


def split_bands(bands, along, offset, after):
    moved = after(bands, along, offset)
    return jnp.concatenate([(bands + moved) * half_root, (bands - moved) * half_root], axis=0)


def merge_bands(bands, along, offset, before):
    half = bands.shape[0] // 2
    lower = bands[:half]
    upper = bands[half:]
    return (lower + upper + before(lower - upper, along, offset)) * quarter_root


def shrink_detail(detail, limit):
    magnitude = jnp.sqrt(detail[:, 0] * detail[:, 0] + detail[:, 1] * detail[:, 1])
    limit = limit.reshape((-1, 1, 1, 1))
    factor = jnp.maximum(magnitude - limit, 0.0) / jnp.maximum(magnitude, limit)
    return detail * factor[:, None]


def wavelet_shrink(descent, thresholds, moves):
    coarse = descent[None]
    details = []
    for level in range(thresholds.shape[0]):
        offset = 2**level
        bands = coarse
        for along, after, before in moves:
            bands = split_bands(bands, along, offset, after)
        coarse = bands[:1]
        details.append(shrink_detail(bands[1:], thresholds[level]))
    for level in reversed(range(thresholds.shape[0])):
        offset = 2**level
        bands = jnp.concatenate([coarse, details[level]], axis=0)
        for along, after, before in reversed(moves):
            bands = merge_bands(bands, along, offset, before)
        coarse = bands
    return coarse[0]


def local(image, sens, measured, mask, thresholds):
    readout_cells = image.shape[3]
    phase_cells = image.shape[1]
    depth_cells = measured.shape[3]
    table_readout = fourier_table(readout_cells, -1.0)
    table_phase = fourier_table(phase_cells, -1.0)
    table_depth = fourier_table(depth_cells, -1.0)
    inverse_readout = fourier_table(readout_cells, 1.0)
    inverse_phase = fourier_table(phase_cells, 1.0)
    inverse_depth = fourier_table(depth_cells, 1.0)
    sens_wide = sens.astype(jnp.float32)
    coil_image = complex_product(sens_wide, image[:, None]).astype(jnp.bfloat16)
    readout_done = contract("tcyzj,stjk->scyzk", coil_image, table_readout).astype(jnp.bfloat16)
    phase_done = contract("tcjzx,stjk->sckzx", readout_done, table_phase).astype(jnp.bfloat16)
    spread = lax.all_to_all(phase_done, ("slab", "row"), split_axis=2, concat_axis=3, tiled=True)
    spectrum = contract("tcyjx,stjk->scykx", spread, table_depth)
    sampled = mask.astype(jnp.float32)[None, None, :, :, None]
    residual = (sampled * (spectrum - measured.astype(jnp.float32))).astype(jnp.bfloat16)
    depth_back = contract("tcyjx,stjk->scykx", residual, inverse_depth).astype(jnp.bfloat16)
    gathered = lax.all_to_all(depth_back, ("slab", "row"), split_axis=3, concat_axis=2, tiled=True)
    phase_back = contract("tcjzx,stjk->sckzx", gathered, inverse_phase).astype(jnp.bfloat16)
    readout_back = contract("tcyzj,stjk->scyzk", phase_back, inverse_readout)
    partial_value = jnp.stack(
        [
            jnp.sum(sens_wide[0] * readout_back[0] + sens_wide[1] * readout_back[1], axis=0),
            jnp.sum(sens_wide[0] * readout_back[1] - sens_wide[1] * readout_back[0], axis=0),
        ]
    )
    gradient = lax.psum(partial_value.astype(jnp.bfloat16), "coil").astype(jnp.float32)
    descent = image - step_size * gradient
    moves = [
        (4, roll_after, roll_before),
        (2, roll_after, roll_before),
        (3, plane_after, plane_before),
    ]
    return wavelet_shrink(descent, thresholds, moves)


def solution(mesh):
    return jax.shard_map(
        local,
        mesh=mesh,
        in_specs=(
            P("groups", None, ("slab", "row"), None),
            P("groups", "coil", None, ("slab", "row"), None),
            P("groups", "coil", ("slab", "row"), None, None),
            P(("slab", "row"), None),
            P(),
        ),
        out_specs=P("groups", None, ("slab", "row"), None),
        check_vma=False,
    )
```

profile of v0, /device:TPU:0, one launch (start us, length us, event | category | flops | bytes accessed | tf_op | source)
XLA Modules:
  0.0 727.4 jit_solution(10082498368846165496)
XLA Ops:
  7.4 11.7 %copy_convert_fusion = f32[2,8,128,16,128]{4,2,0,3,1:T(8,128)} fusion(bf16[2,8,128,16,128]{4,3,2,1,0:T(8,128)(2,1)} %param.6), kind=kLoop, calls=%fused_computation.53 | loop fusion | flops 4194304 | bytes 25165824 | tf_op jit(solution)/shard_map/convert_element_type | solution.py:111
  20.0 9.9 %subtract_convert_fusion = (bf16[1,8,128,16,128]{4,2,0,3,1:T(8,128)(2,1)}, bf16[1,8,128,16,128]{4,2,0,3,1:T(8,128)(2,1)}) fusion(f32[2,8,128,16,128]{4,2,0,3,1:T(8,128)} %copy_convert_fusion, f32[128,16,128]{2,0,1:T(8,128)S(1)} %copy.36, f32[128,16,128]{2,0,1:T(8,128)S(1)} %copy.35), kind=kLoop, calls=%fused_computation.61 | loop fusion | flops 16777216 | bytes 27262976 | tf_op jit(solution)/shard_map/convert.8
  29.9 9.1 %fusion.6 = bf16[2,8,128,16,128]{4,2,3,1,0:T(8,128)(2,1)} fusion(bf16[1,8,128,16,128]{4,2,0,3,1:T(8,128)(2,1)} %get-tuple-element.8, bf16[1,8,128,16,128]{4,2,0,3,1:T(8,128)(2,1)} %get-tuple-element.7, bf16[1,2,128,128]{2,3,1,0:T(8,128)(2,1)S(1)} %get-tuple-element.28, bf16[1,2,128,128]{2,3,1,0:T(8,128)(2,1)S(1)} %get-tuple-element.29), kind=kOutput, calls=%fused_computation.30 | convolution fusion | flops 4320657408 | bytes 16908288 | tf_op jit(solution)/shard_map/tcjzx,stjk->sckzx/dot_general | solution.py:31
  39.0 12.0 %copy.38 = bf16[2,8,128,16,128]{4,3,1,0,2:T(8,128)(2,1)} copy(bf16[2,8,128,16,128]{4,2,3,1,0:T(8,128)(2,1)} %fusion.6) | data formatting | bytes 16777216 | tf_op jit(solution)/shard_map/convert_element_type | solution.py:114
  51.0 7.6 %all-to-all-start = ((bf16[2,8,128,16,128]{4,3,1,0,2:T(8,128)(2,1)}), bf16[2,8,128,16,128]{4,3,1,0,2:T(8,128)(2,1)}, u32[]{:S(2)}, u32[]{:S(2)}) async-start(bf16[2,8,128,16,128]{4,3,1,0,2:T(8,128)(2,1)} %copy.38), calls=%async_computation | async-start | bytes 16777216 | tf_op jit(solution)/shard_map/all_to_all | solution.py:115
  62.0 147.1 %all-to-all-done = bf16[2,8,128,16,128]{4,3,1,0,2:T(8,128)(2,1)} async-done(((bf16[2,8,128,16,128]{4,3,1,0,2:T(8,128)(2,1)}), bf16[2,8,128,16,128]{4,3,1,0,2:T(8,128)(2,1)}, u32[]{:S(2)}, u32[]{:S(2)}) %all-to-all-start) | async-done | bytes 8388640 | tf_op jit(solution)/shard_map/all_to_all | solution.py:115
  209.2 9.1 %copy.40 = bf16[2,8,8,16,16,128]{5,4,3,2,1,0:T(8,128)(2,1)} copy(bf16[2,8,8,16,16,128]{5,4,1,0,2,3:T(8,128)(2,1)} %bitcast.31) | data formatting | bytes 16777216 | tf_op jit(solution)/shard_map/all_to_all | solution.py:115
  218.3 9.5 %fusion.1 = bf16[2,8,8,256,128]{4,3,2,1,0:T(8,128)(2,1)S(1)} fusion(bf16[2,8,8,256,128]{4,3,2,1,0:T(8,128)(2,1)} %param.7, f32[8,256]{1,0:T(8,128)S(1)} %convert_element_type.150, bf16[2,8,8,256,128]{4,3,2,1,0:T(8,128)(2,1)} %bitcast.172, bf16[1,2,256,256]{2,3,1,0:T(8,128)(2,1)S(1)} %get-tuple-element.24, bf16[1,2,256,256]{2,3,1,0:T(8,128)(2,1)S(1)} %get-tuple-element.25), kind=kOutput, calls=%fused_computation.10 | convolution fusion | flops 4312793088 | bytes 25698304 | tf_op jit(solution)/shard_map/tcyjx,stjk->scykx/dot_general | solution.py:31
  234.6 12.1 %copy.43 = bf16[2,8,8,256,128]{4,2,1,0,3:T(8,128)(2,1)} copy(bf16[2,8,8,256,128]{4,3,2,1,0:T(8,128)(2,1)} %fusion.7) | data formatting | bytes 16777216 | tf_op jit(solution)/shard_map/convert_element_type | solution.py:119
  246.6 218.8 %all_to_all.36 = bf16[2,8,8,256,128]{4,2,1,0,3:T(8,128)(2,1)} all-to-all(bf16[2,8,8,256,128]{4,2,1,0,3:T(8,128)(2,1)} %copy.43), channel_id=1, replica_groups=mesh['groups'=1,'slab'=8,'coil'=2,'row'=2] {'slab','row'}, dimensions={3} | all-to-all | bytes 16777216 | tf_op jit(solution)/shard_map/all_to_all | solution.py:120
  465.4 16.3 %copy.45 = bf16[2,8,16,8,16,128]{5,4,3,2,1,0:T(8,128)(2,1)} copy(bf16[2,8,16,8,16,128]{5,3,1,0,4,2:T(8,128)(2,1)} %bitcast.169) | data formatting | bytes 16777216 | tf_op jit(solution)/shard_map/all_to_all | solution.py:120
  481.8 12.5 %convolution_bitcast_fusion = f32[2,8,128,16,128]{4,2,0,3,1:T(8,128)} fusion(bf16[2,8,128,16,128,1]{4,3,2,1,0,5:T(8,128)(2,1)} %bitcast.168, bf16[1,2,128,128]{2,3,1,0:T(8,128)(2,1)S(1)} %get-tuple-element.30, bf16[1,2,128,128]{2,3,1,0:T(8,128)(2,1)S(1)} %get-tuple-element.27), kind=kOutput, calls=%fused_computation.29 | convolution fusion | flops 4299685888 | bytes 25296896 | tf_op jit(solution)/shard_map/tcyzj,stjk->scyzk/dot_general | solution.py:31
  494.3 13.1 %add_reduce_fusion = (bf16[128,16,128]{2,0,1:T(8,128)(2,1)S(1)}, bf16[128,16,128]{2,0,1:T(8,128)(2,1)S(1)}) fusion(f32[2,8,128,16,128]{4,2,0,3,1:T(8,128)} %convolution_bitcast_fusion, f32[2,8,128,16,128]{4,2,0,3,1:T(8,128)} %copy_convert_fusion), kind=kLoop, calls=%fused_computation.59 | loop fusion | flops 16252928 | bytes 34603008 | tf_op jit(solution)/shard_map/reduce_sum | solution.py:125
  511.1 39.3 %all-reduce.2.cloned.1.call-done = bf16[2,128,16,128]{1,3,2,0:T(8,128)(2,1)} async-done(((bf16[2,128,16,128]{1,3,2,0:T(8,128)(2,1)}), bf16[2,128,16,128]{1,3,2,0:T(8,128)(2,1)}) %all-reduce.2.cloned.1.call-update) | async-done | bytes 1048592 | tf_op jit(solution)/shard_map/psum | solution.py:129
  564.1 6.8 subtract_multiply_fusion
  596.3 8.9 %subtract_multiply_fusion.1 = (f32[4,2,128,16,128]{2,4,3,1,0:T(8,128)}, f32[4,2,128,16,128]{2,4,3,1,0:T(8,128)S(1)}) fusion(f32[4,2,128,2,128]{2,4,3,1,0:T(8,128)S(1)} %convert_element_type.163, f32[4,2,128,14,128]{2,4,3,1,0:T(8,128)} %fusion.23, f32[2,2,128,16,128]{2,4,3,1,0:T(8,128)} %copy-done.4, f32[2,2,128,16,128]{2,4,3,1,0:T(8,128)} %copy-done.5), kind=kLoop, calls=%fused_computation.55 | loop fusion | flops 12582912 | bytes 33554432 | tf_op jit(solution)/shard_map/mul | solution.py:65
  608.4 7.7 %divide_bitcast_fusion.1 = f32[7,128,16,128]{1,3,2,0:T(8,128)} fusion(f32[4,2,128,16,128]{2,4,3,1,0:T(8,128)} %get-tuple-element.9, f32[4,2,128,16,128]{2,4,3,1,0:T(8,128)S(1)} %get-tuple-element.10, f32[7]{0:T(128)S(1)} %get-tuple-element.31), kind=kLoop, calls=%fused_computation.79 | loop fusion | flops 16515072 | bytes 24117276 | tf_op jit(solution)/shard_map/mul | solution.py:79
  616.2 8.2 %fusion.5 = f32[7,2,128,16,128]{2,4,3,1,0:T(8,128)S(1)} fusion(f32[4,2,128,16,128]{2,4,3,1,0:T(8,128)} %copy-done.1, f32[4,2,128,16,128]{2,4,3,1,0:T(8,128)} %get-tuple-element.9, f32[7,128,16,128]{1,3,2,0:T(8,128)} %divide_bitcast_fusion.1), kind=kLoop, calls=%fused_computation.18 | loop fusion | flops 7340032 | bytes 38797312 | tf_op jit(solution)/shard_map/mul | solution.py:79
  629.8 11.4 %fusion.3 = f32[7,2,128,16,128]{2,4,3,1,0:T(8,128)} fusion(f32[4,2,128,16,128]{2,4,3,1,0:T(8,128)S(1)} %bitcast.165, f32[4,2,128,16,128]{2,4,3,1,0:T(8,128)} %copy-done.3, f32[7,128,16,128]{1,3,2,0:T(8,128)} %divide_bitcast_fusion), kind=kLoop, calls=%fused_computation.16 | loop fusion | flops 7340032 | bytes 38797312 | tf_op jit(solution)/shard_map/mul | solution.py:79
  641.3 6.9 slice.282
  648.3 6.9 fusion.10
  662.7 9.9 %fusion.44 = f32[2,2,128,16,128]{2,4,3,1,0:T(8,128)} fusion(f32[2,2,126,16,128]{2,4,3,1,0:T(8,128)} %bitcast.166, f32[2,2,2,16,128]{2,4,3,1,0:T(8,128)} %slice.285, f32[4,2,128,16,128]{2,4,3,1,0:T(8,128)} %fusion.10), kind=kLoop, calls=%fused_computation.97 | loop fusion | flops 4194304 | bytes 16777216 | tf_op jit(solution)/shard_map/mul | solution.py:72
  683.5 7.3 %slice.297 = f32[4,2,128,15,128]{2,4,3,1,0:T(8,128)} slice(f32[4,2,128,16,128]{2,4,3,1,0:T(8,128)} %copy-done.10), slice={[0:4], [0:2], [0:128], [0:15], [0:128]} | slice | bytes 15728640 | tf_op jit(solution)/shard_map/slice | solution.py:59
  692.0 7.2 fusion.11
  (111 shorter events, 103.6 us)
Async XLA Ops:
  7.4 11.7 %copy-start.11 = (f32[2,128,16,128]{3,2,1,0:T(8,128)S(1)}, f32[2,128,16,128]{3,2,1,0:T(8,128)}, u32[]{:S(2)}) copy-start(f32[2,128,16,128]{3,2,1,0:T(8,128)} %param.5) | copy-start | bytes 6291460
  51.0 7.7 %copy-start.13 = (s32[8,256]{1,0:T(8,128)S(1)}, s32[8,256]{1,0:T(8,128)}, u32[]{:S(2)}) copy-start(s32[8,256]{1,0:T(8,128)} %param.8) | copy-start | bytes 24580
  51.0 158.2 %all-to-all-start = ((bf16[2,8,128,16,128]{4,3,1,0,2:T(8,128)(2,1)}), bf16[2,8,128,16,128]{4,3,1,0,2:T(8,128)(2,1)}, u32[]{:S(2)}, u32[]{:S(2)}) async-start(bf16[2,8,128,16,128]{4,3,1,0,2:T(8,128)(2,1)} %copy.38), calls=%async_computation | async-start | bytes 16777216 | tf_op jit(solution)/shard_map/all_to_all | solution.py:115
  58.6 491.8 %all-reduce.2.cloned.1.call-start = ((), (), s32[]{:S(2)}) async-start(), calls=%async_computation.2 | async-start | bytes 2097152 | tf_op jit(solution)/shard_map/psum | solution.py:129
  507.4 3.7 copy-start.14
  556.5 7.4 %copy-start.6 = (f32[2,2,128,16,128]{2,4,3,1,0:T(8,128)}, f32[2,2,128,16,128]{2,4,3,1,0:T(8,128)S(1)}, u32[]{:S(2)}) copy-start(f32[2,2,128,16,128]{2,4,3,1,0:T(8,128)S(1)} %get-tuple-element.15) | copy-start | bytes 12582916
  556.5 7.4 %copy-start.7 = (f32[2,2,128,16,128]{2,4,3,1,0:T(8,128)}, f32[2,2,128,16,128]{2,4,3,1,0:T(8,128)S(1)}, u32[]{:S(2)}) copy-start(f32[2,2,128,16,128]{2,4,3,1,0:T(8,128)S(1)} %get-tuple-element.16) | copy-start | bytes 12582916
  556.6 7.5 %collective-permute-start = (bf16[4,2,128,1,128]{2,4,3,1,0:T(8,128)(2,1)S(1)}, bf16[4,2,128,1,128]{2,4,3,1,0:T(8,128)(2,1)S(1)}, u32[]{:S(2)}, u32[]{:S(2)}) collective-permute-start(bf16[4,2,128,1,128]{2,4,3,1,0:T(8,128)(2,1)S(1)} %fusion.61), channel_id=1, source_target_pairs={{1,0},{4,1},{5,4},{8,5},{9,8},{12,9},{13,12},{16,13},{17,16},{20,1... | collective-permute-start | bytes 786440 | tf_op jit(solution)/shard_map/ppermute | solution.py:15
  570.9 16.8 %copy-start = (f32[4,2,128,16,128]{2,4,3,1,0:T(8,128)}, f32[4,2,128,16,128]{2,4,3,1,0:T(8,128)S(1)}, u32[]{:S(2)}) copy-start(f32[4,2,128,16,128]{2,4,3,1,0:T(8,128)S(1)} %get-tuple-element.12) | copy-start | bytes 25165828
  570.9 16.8 %copy-start.3 = (f32[4,2,128,16,128]{2,4,3,1,0:T(8,128)}, f32[4,2,128,16,128]{2,4,3,1,0:T(8,128)S(1)}, u32[]{:S(2)}) copy-start(f32[4,2,128,16,128]{2,4,3,1,0:T(8,128)S(1)} %get-tuple-element.11) | copy-start | bytes 25165828
  582.9 10.1 %copy-start.4 = (f32[2,2,128,16,128]{2,4,3,1,0:T(8,128)}, f32[2,2,128,16,128]{2,4,3,1,0:T(8,128)S(1)}, u32[]{:S(2)}) copy-start(f32[2,2,128,16,128]{2,4,3,1,0:T(8,128)S(1)} %get-tuple-element.13) | copy-start | bytes 12582916
  582.9 10.1 %copy-start.5 = (f32[2,2,128,16,128]{2,4,3,1,0:T(8,128)}, f32[2,2,128,16,128]{2,4,3,1,0:T(8,128)S(1)}, u32[]{:S(2)}) copy-start(f32[2,2,128,16,128]{2,4,3,1,0:T(8,128)S(1)} %get-tuple-element.14) | copy-start | bytes 12582916
  583.0 13.2 %collective-permute-start.1 = (bf16[4,2,128,2,128]{2,4,3,1,0:T(8,128)(2,1)S(1)}, bf16[4,2,128,2,128]{2,4,3,1,0:T(8,128)(2,1)S(1)}, u32[]{:S(2)}, u32[]{:S(2)}) collective-permute-start(bf16[4,2,128,2,128]{2,4,3,1,0:T(8,128)(2,1)S(1)} %fusion.54), channel_id=1, source_target_pairs={{1,0},{4,1},{5,4},{8,5},{9,8},{12,9},{13,12},{16,13},{17,16},{20,1... | collective-permute-start | bytes 1572872 | tf_op jit(solution)/shard_map/ppermute | solution.py:15
  608.4 21.4 %slice-start.4 = ((s8[8388608]{0:T(1024)(128)(4,1)}), s8[4194304]{0:T(1024)(128)(4,1)S(1)}, s32[]{:S(2)}) async-start(s8[8388608]{0:T(1024)(128)(4,1)} %bitcast.164), calls=%async_computation.7 | async-start | bytes 8388608
  616.2 13.6 %slice-start.5 = ((s8[8388608]{0:T(1024)(128)(4,1)}), s8[4194304]{0:T(1024)(128)(4,1)S(1)}, s32[]{:S(2)}) async-start(s8[8388608]{0:T(1024)(128)(4,1)} %bitcast.164), calls=%async_computation.8 | async-start | bytes 8388608
  629.7 18.5 %collective-permute-start.2 = (bf16[4,2,128,2,128]{2,4,3,1,0:T(8,128)(2,1)S(1)}, bf16[4,2,128,2,128]{2,4,3,1,0:T(8,128)(2,1)S(1)}, u32[]{:S(2)}, u32[]{:S(2)}) collective-permute-start(bf16[4,2,128,2,128]{2,4,3,1,0:T(8,128)(2,1)S(1)} %slice.450), channel_id=1, source_target_pairs={{29,0},{0,1},{1,4},{4,5},{5,8},{8,9},{9,12},{12,13},{13,16},{16,17... | collective-permute-start | bytes 1572872 | tf_op jit(solution)/shard_map/ppermute | solution.py:15
  662.7 15.5 %slice-start = ((s8[14680064]{0:T(1024)(128)(4,1)}), s8[4194304]{0:T(1024)(128)(4,1)S(1)}, s32[]{:S(2)}) async-start(s8[14680064]{0:T(1024)(128)(4,1)} %bitcast.162), calls=%async_computation.3 | async-start | bytes 8388608
  662.7 15.5 %slice-start.1 = ((s8[14680064]{0:T(1024)(128)(4,1)}), s8[4194304]{0:T(1024)(128)(4,1)S(1)}, s32[]{:S(2)}) async-start(s8[14680064]{0:T(1024)(128)(4,1)} %bitcast.162), calls=%async_computation.4 | async-start | bytes 8388608
  662.7 15.6 %slice-start.2 = ((s8[14680064]{0:T(1024)(128)(4,1)}), s8[2097152]{0:T(1024)(128)(4,1)S(1)}, s32[]{:S(2)}) async-start(s8[14680064]{0:T(1024)(128)(4,1)} %bitcast.162), calls=%async_computation.5 | async-start | bytes 4194304
  672.6 5.6 slice-start.3
  680.1 3.3 copy-start.10
  683.4 8.5 %collective-permute-start.3 = (bf16[4,2,128,1,128]{2,4,3,1,0:T(8,128)(2,1)S(1)}, bf16[4,2,128,1,128]{2,4,3,1,0:T(8,128)(2,1)S(1)}, u32[]{:S(2)}, u32[]{:S(2)}) collective-permute-start(bf16[4,2,128,1,128]{2,4,3,1,0:T(8,128)(2,1)S(1)} %slice.451), channel_id=1, source_target_pairs={{29,0},{0,1},{1,4},{4,5},{5,8},{8,9},{9,12},{12,13},{13,16},{16,17... | collective-permute-start | bytes 786440 | tf_op jit(solution)/shard_map/ppermute | solution.py:15
  703.4 4.9 copy-start.2
  714.0 3.4 copy-start.9
  (3 other events, 8.3 us)
Sparse Core Ops, SparseCore 0:
  509.2 41.1 all-reduce.1
where the time goes:
time: 731 us; the launch traced here: 727 us
  blocking collectives  219 us (30%)
  waiting for transfers between devices  188 us (26%)
  other arithmetic  166 us (23%)
  local copies, waits for them, and re-layouts  86.6 us (12%)
  matrix products  37.9 us (5%)
  starting transfers between devices  16 us (2%)
  between operations  14.2 us (2%)
    all_to_all x1, blocking collectives, local(): lax.all_to_all(depth_back, ('slab', 'row'), split_axis=3, concat_axis=2,...  219 us
    all_to_all x1, waiting for transfers between devices, local(): lax.all_to_all(phase_done, ('slab', 'row'), split_axis=2, concat_axis=3,...  147 us
    psum x1, waiting for transfers between devices, local(): lax.psum(partial_value.astype(jnp.bfloat16), 'coil').astype(jnp.float32)  39.3 us
    dot_general x4, matrix products, contract(): return jnp.einsum(form, values, table, preferred_element_type=jnp.float32)  37.9 us
    mul x4, other arithmetic, shrink_detail(): return detail * factor[:, None]  32.8 us
    mul x5, other arithmetic, merge_bands(): return (lower + upper + before(lower - upper, along, offset)) * quarter_root  32.6 us
    mul x3, other arithmetic, split_bands(): (bands - moved) * half_root  19.9 us
    sub x6, other arithmetic, merge_bands(): return (lower + upper + before(lower - upper, along, offset)) * quarter_root  19.6 us
  transfers between devices with their start and end apart: 6, of which 4 were waited for; matrix products, arithmetic and copies ran while one was open for 6% of the time, Pallas kernels for 0%

commit v1 on v0

--- a/solution.py
+++ b/solution.py
@@ -112,7 +112,16 @@
     coil_image = complex_product(sens_wide, image[:, None]).astype(jnp.bfloat16)
     readout_done = contract("tcyzj,stjk->scyzk", coil_image, table_readout).astype(jnp.bfloat16)
     phase_done = contract("tcjzx,stjk->sckzx", readout_done, table_phase).astype(jnp.bfloat16)
-    spread = lax.all_to_all(phase_done, ("slab", "row"), split_axis=2, concat_axis=3, tiled=True)
+    lead_keys = lambda arr_in: jnp.concatenate(
+        lax.all_to_all(
+            jnp.stack(jnp.split(arr_in, lax.axis_size(("slab", "row")), axis=2)),
+            ("slab", "row"),
+            0,
+            0,
+        ),
+        axis=3,
+    )
+    spread = lead_keys(phase_done)
     spectrum = contract("tcyjx,stjk->scykx", spread, table_depth)
     sampled = mask.astype(jnp.float32)[None, None, :, :, None]
     residual = (sampled * (spectrum - measured.astype(jnp.float32))).astype(jnp.bfloat16)

time: 731 us -> 753 us (1.030)
  local copies, waits for them, and re-layouts: 86.6 us -> 105 us
    unnamed x45 -> x60, local copies, waits for them, and re-layouts: 11.3 us -> 39.7 us
    convert_element_type x1 -> x0, local copies, waits for them, and re-layouts: 12 us -> none  [local(): contract('tcjzx,stjk->sckzx', readout_done, table_phase)]
    all_to_all x1 -> x0, local copies, waits for them, and re-layouts: 9.14 us -> none  [local(): lax.all_to_all(phase_done, ('slab', 'row'), split_axis=2, concat_axis=3,...]
    reshape x0 -> x1, local copies, waits for them, and re-layouts: none -> 9.09 us  [local(): jnp.concatenate(lax.all_to_all(jnp.stack(jnp.split(arr_in, lax.axis_size(...]
  transfers between devices with their start and end apart: 6 -> 6, of which waited for: 4 -> 3; matrix products, arithmetic and copies ran while one was open for 6% -> 6% of each run, Pallas kernels for 0% -> 0%
where the time goes in v1:
time: 753 us; the launch traced here: 745 us
  blocking collectives  219 us (29%)
  waiting for transfers between devices  187 us (25%)
  other arithmetic  166 us (22%)
  local copies, waits for them, and re-layouts  105 us (14%)
  matrix products  38.2 us (5%)
  starting transfers between devices  16.1 us (2%)
  between operations  14.2 us (2%)
    all_to_all x1, blocking collectives, local(): lax.all_to_all(depth_back, ('slab', 'row'), split_axis=3, concat_axis=2,...  219 us
    all_to_all x1, waiting for transfers between devices, local(): lax.all_to_all(jnp.stack(jnp.split(arr_in, lax.axis_size(('slab', 'row'))...  147 us
    unnamed x60, local copies, waits for them, and re-layouts  39.7 us
    psum x1, waiting for transfers between devices, local(): lax.psum(partial_value.astype(jnp.bfloat16), 'coil').astype(jnp.float32)  39.3 us
    dot_general x4, matrix products, contract(): return jnp.einsum(form, values, table, preferred_element_type=jnp.float32)  38.2 us
    mul x4, other arithmetic, shrink_detail(): return detail * factor[:, None]  32.7 us
    mul x5, other arithmetic, merge_bands(): return (lower + upper + before(lower - upper, along, offset)) * quarter_root  32.6 us
    mul x3, other arithmetic, split_bands(): (bands - moved) * half_root  19.9 us
  transfers between devices with their start and end apart: 6, of which 3 were waited for; matrix products, arithmetic and copies ran while one was open for 6% of the time, Pallas kernels for 0%

profile of v1, /device:TPU:0, one launch (start us, length us, event | category | flops | bytes accessed | tf_op | source)
XLA Modules:
  0.0 745.3 jit_solution(6939945134582914592)
XLA Ops:
  7.4 11.7 %copy_convert_fusion = f32[2,8,128,16,128]{4,2,0,3,1:T(8,128)} fusion(bf16[2,8,128,16,128]{4,3,2,1,0:T(8,128)(2,1)} %param.6), kind=kLoop, calls=%fused_computation.53 | loop fusion | flops 4194304 | bytes 25165824 | tf_op jit(solution)/shard_map/convert_element_type | solution.py:111
  20.0 9.4 %subtract_convert_fusion = (bf16[1,8,128,16,128]{4,2,0,3,1:T(8,128)(2,1)}, bf16[1,8,128,16,128]{4,2,0,3,1:T(8,128)(2,1)}) fusion(f32[2,8,128,16,128]{4,2,0,3,1:T(8,128)} %copy_convert_fusion, f32[128,16,128]{2,0,1:T(8,128)S(1)} %copy.36, f32[128,16,128]{2,0,1:T(8,128)S(1)} %copy.35), kind=kLoop, calls=%fused_computation.61 | loop fusion | flops 16777216 | bytes 27262976 | tf_op jit(solution)/shard_map/convert.8
  29.4 9.1 %fusion.6 = bf16[2,8,128,16,128]{4,2,3,1,0:T(8,128)(2,1)} fusion(bf16[1,8,128,16,128]{4,2,0,3,1:T(8,128)(2,1)} %get-tuple-element.8, bf16[1,8,128,16,128]{4,2,0,3,1:T(8,128)(2,1)} %get-tuple-element.7, bf16[1,2,128,128]{2,3,1,0:T(8,128)(2,1)S(1)} %get-tuple-element.28, bf16[1,2,128,128]{2,3,1,0:T(8,128)(2,1)S(1)} %get-tuple-element.29), kind=kOutput, calls=%fused_computation.30 | convolution fusion | flops 4320657408 | bytes 16908288 | tf_op jit(solution)/shard_map/tcjzx,stjk->sckzx/dot_general | solution.py:31
  68.8 7.6 %all-to-all-start = ((bf16[16,2,8,8,16,128]{5,3,4,2,1,0:T(8,128)(2,1)}), bf16[16,2,8,8,16,128]{5,3,4,2,1,0:T(8,128)(2,1)}, u32[]{:S(2)}, u32[]{:S(2)}) async-start(bf16[16,2,8,8,16,128]{5,3,4,2,1,0:T(8,128)(2,1)} %fusion.57), calls=%async_computation | async-start | bytes 16777216 | tf_op jit(solution)/shard_map/all_to_all | solution.py:116
  80.0 147.0 %all-to-all-done = bf16[16,2,8,8,16,128]{5,3,4,2,1,0:T(8,128)(2,1)} async-done(((bf16[16,2,8,8,16,128]{5,3,4,2,1,0:T(8,128)(2,1)}), bf16[16,2,8,8,16,128]{5,3,4,2,1,0:T(8,128)(2,1)}, u32[]{:S(2)}, u32[]{:S(2)}) %all-to-all-start) | async-done | bytes 8388640 | tf_op jit(solution)/shard_map/all_to_all | solution.py:116
  227.0 9.1 %copy.38 = bf16[2,8,8,16,16,128]{5,4,3,2,1,0:T(8,128)(2,1)} copy(bf16[2,8,8,16,16,128]{5,2,4,1,0,3:T(8,128)(2,1)} %bitcast.45) | data formatting | bytes 16777216 | tf_op jit(solution)/shard_map/reshape | solution.py:115
  236.1 9.5 %fusion.1 = bf16[2,8,8,256,128]{4,3,2,1,0:T(8,128)(2,1)S(1)} fusion(bf16[2,8,8,256,128]{4,3,2,1,0:T(8,128)(2,1)} %param.7, f32[8,256]{1,0:T(8,128)S(1)} %convert_element_type.150, bf16[2,8,8,256,128]{4,3,2,1,0:T(8,128)(2,1)} %bitcast.234, bf16[1,2,256,256]{2,3,1,0:T(8,128)(2,1)S(1)} %get-tuple-element.24, bf16[1,2,256,256]{2,3,1,0:T(8,128)(2,1)S(1)} %get-tuple-element.25), kind=kOutput, calls=%fused_computation.10 | convolution fusion | flops 4312793088 | bytes 25698304 | tf_op jit(solution)/shard_map/tcyjx,stjk->scykx/dot_general | solution.py:31
  245.6 7.2 fusion.7
  252.8 12.1 %copy.41 = bf16[2,8,8,256,128]{4,2,1,0,3:T(8,128)(2,1)} copy(bf16[2,8,8,256,128]{4,3,2,1,0:T(8,128)(2,1)} %fusion.7) | data formatting | bytes 16777216 | tf_op jit(solution)/shard_map/convert_element_type | solution.py:128
  264.9 218.8 %all_to_all.23 = bf16[2,8,8,256,128]{4,2,1,0,3:T(8,128)(2,1)} all-to-all(bf16[2,8,8,256,128]{4,2,1,0,3:T(8,128)(2,1)} %copy.41), channel_id=1, replica_groups=mesh['groups'=1,'slab'=8,'coil'=2,'row'=2] {'slab','row'}, dimensions={3} | all-to-all | bytes 16777216 | tf_op jit(solution)/shard_map/all_to_all | solution.py:129
  483.6 16.3 %copy.43 = bf16[2,8,16,8,16,128]{5,4,3,2,1,0:T(8,128)(2,1)} copy(bf16[2,8,16,8,16,128]{5,3,1,0,4,2:T(8,128)(2,1)} %bitcast.231) | data formatting | bytes 16777216 | tf_op jit(solution)/shard_map/all_to_all | solution.py:129
  500.0 12.3 %convolution_bitcast_fusion = f32[2,8,128,16,128]{4,2,0,3,1:T(8,128)} fusion(bf16[2,8,128,16,128,1]{4,3,2,1,0,5:T(8,128)(2,1)} %bitcast.230, bf16[1,2,128,128]{2,3,1,0:T(8,128)(2,1)S(1)} %get-tuple-element.30, bf16[1,2,128,128]{2,3,1,0:T(8,128)(2,1)S(1)} %get-tuple-element.27), kind=kOutput, calls=%fused_computation.29 | convolution fusion | flops 4299685888 | bytes 25296896 | tf_op jit(solution)/shard_map/tcyzj,stjk->scyzk/dot_general | solution.py:31
  512.3 13.1 %add_reduce_fusion = (bf16[128,16,128]{2,0,1:T(8,128)(2,1)S(1)}, bf16[128,16,128]{2,0,1:T(8,128)(2,1)S(1)}) fusion(f32[2,8,128,16,128]{4,2,0,3,1:T(8,128)} %convolution_bitcast_fusion, f32[2,8,128,16,128]{4,2,0,3,1:T(8,128)} %copy_convert_fusion), kind=kLoop, calls=%fused_computation.59 | loop fusion | flops 16252928 | bytes 34603008 | tf_op jit(solution)/shard_map/reduce_sum | solution.py:134
  529.1 39.3 %all-reduce.2.cloned.1.call-done = bf16[2,128,16,128]{1,3,2,0:T(8,128)(2,1)} async-done(((bf16[2,128,16,128]{1,3,2,0:T(8,128)(2,1)}), bf16[2,128,16,128]{1,3,2,0:T(8,128)(2,1)}) %all-reduce.2.cloned.1.call-update) | async-done | bytes 1048592 | tf_op jit(solution)/shard_map/psum | solution.py:138
  582.2 6.8 subtract_multiply_fusion
  614.4 8.9 %subtract_multiply_fusion.1 = (f32[4,2,128,16,128]{2,4,3,1,0:T(8,128)}, f32[4,2,128,16,128]{2,4,3,1,0:T(8,128)S(1)}) fusion(f32[4,2,128,2,128]{2,4,3,1,0:T(8,128)S(1)} %convert_element_type.163, f32[4,2,128,14,128]{2,4,3,1,0:T(8,128)} %fusion.23, f32[2,2,128,16,128]{2,4,3,1,0:T(8,128)} %copy-done.4, f32[2,2,128,16,128]{2,4,3,1,0:T(8,128)} %copy-done.5), kind=kLoop, calls=%fused_computation.55 | loop fusion | flops 12582912 | bytes 33554432 | tf_op jit(solution)/shard_map/mul | solution.py:65
  626.5 7.7 %divide_bitcast_fusion.1 = f32[7,128,16,128]{1,3,2,0:T(8,128)} fusion(f32[4,2,128,16,128]{2,4,3,1,0:T(8,128)} %get-tuple-element.9, f32[4,2,128,16,128]{2,4,3,1,0:T(8,128)S(1)} %get-tuple-element.10, f32[7]{0:T(128)S(1)} %get-tuple-element.31), kind=kLoop, calls=%fused_computation.79 | loop fusion | flops 16515072 | bytes 24117276 | tf_op jit(solution)/shard_map/mul | solution.py:79
  634.2 8.2 %fusion.5 = f32[7,2,128,16,128]{2,4,3,1,0:T(8,128)S(1)} fusion(f32[4,2,128,16,128]{2,4,3,1,0:T(8,128)} %copy-done.1, f32[4,2,128,16,128]{2,4,3,1,0:T(8,128)} %get-tuple-element.9, f32[7,128,16,128]{1,3,2,0:T(8,128)} %divide_bitcast_fusion.1), kind=kLoop, calls=%fused_computation.18 | loop fusion | flops 7340032 | bytes 38797312 | tf_op jit(solution)/shard_map/mul | solution.py:79
  647.9 11.4 %fusion.3 = f32[7,2,128,16,128]{2,4,3,1,0:T(8,128)} fusion(f32[4,2,128,16,128]{2,4,3,1,0:T(8,128)S(1)} %bitcast.227, f32[4,2,128,16,128]{2,4,3,1,0:T(8,128)} %copy-done.3, f32[7,128,16,128]{1,3,2,0:T(8,128)} %divide_bitcast_fusion), kind=kLoop, calls=%fused_computation.16 | loop fusion | flops 7340032 | bytes 38797312 | tf_op jit(solution)/shard_map/mul | solution.py:79
  659.3 6.9 slice.282
  666.3 6.9 fusion.10
  680.7 9.9 %fusion.44 = f32[2,2,128,16,128]{2,4,3,1,0:T(8,128)} fusion(f32[2,2,126,16,128]{2,4,3,1,0:T(8,128)} %bitcast.228, f32[2,2,2,16,128]{2,4,3,1,0:T(8,128)} %slice.285, f32[4,2,128,16,128]{2,4,3,1,0:T(8,128)} %fusion.10), kind=kLoop, calls=%fused_computation.97 | loop fusion | flops 4194304 | bytes 16777216 | tf_op jit(solution)/shard_map/mul | solution.py:72
  701.5 7.3 slice.297
  710.0 7.2 fusion.11
  (126 shorter events, 127.3 us)
Async XLA Ops:
  7.4 11.7 %copy-start.11 = (f32[2,128,16,128]{3,2,1,0:T(8,128)S(1)}, f32[2,128,16,128]{3,2,1,0:T(8,128)}, u32[]{:S(2)}) copy-start(f32[2,128,16,128]{3,2,1,0:T(8,128)} %param.5) | copy-start | bytes 6291460
  68.8 8.0 %copy-start.13 = (s32[8,256]{1,0:T(8,128)S(1)}, s32[8,256]{1,0:T(8,128)}, u32[]{:S(2)}) copy-start(s32[8,256]{1,0:T(8,128)} %param.8) | copy-start | bytes 24580
  68.8 158.2 %all-to-all-start = ((bf16[16,2,8,8,16,128]{5,3,4,2,1,0:T(8,128)(2,1)}), bf16[16,2,8,8,16,128]{5,3,4,2,1,0:T(8,128)(2,1)}, u32[]{:S(2)}, u32[]{:S(2)}) async-start(bf16[16,2,8,8,16,128]{5,3,4,2,1,0:T(8,128)(2,1)} %fusion.57), calls=%async_computation | async-start | bytes 16777216 | tf_op jit(solution)/shard_map/all_to_all | solution.py:116
  76.4 492.0 %all-reduce.2.cloned.1.call-start = ((), (), s32[]{:S(2)}) async-start(), calls=%async_computation.2 | async-start | bytes 2097152 | tf_op jit(solution)/shard_map/psum | solution.py:138
  525.4 3.7 copy-start.14
  574.5 7.6 %copy-start.6 = (f32[2,2,128,16,128]{2,4,3,1,0:T(8,128)}, f32[2,2,128,16,128]{2,4,3,1,0:T(8,128)S(1)}, u32[]{:S(2)}) copy-start(f32[2,2,128,16,128]{2,4,3,1,0:T(8,128)S(1)} %get-tuple-element.15) | copy-start | bytes 12582916
  574.6 7.6 %copy-start.7 = (f32[2,2,128,16,128]{2,4,3,1,0:T(8,128)}, f32[2,2,128,16,128]{2,4,3,1,0:T(8,128)S(1)}, u32[]{:S(2)}) copy-start(f32[2,2,128,16,128]{2,4,3,1,0:T(8,128)S(1)} %get-tuple-element.16) | copy-start | bytes 12582916
  574.6 7.6 %collective-permute-start = (bf16[4,2,128,1,128]{2,4,3,1,0:T(8,128)(2,1)S(1)}, bf16[4,2,128,1,128]{2,4,3,1,0:T(8,128)(2,1)S(1)}, u32[]{:S(2)}, u32[]{:S(2)}) collective-permute-start(bf16[4,2,128,1,128]{2,4,3,1,0:T(8,128)(2,1)S(1)} %fusion.77), channel_id=1, source_target_pairs={{1,0},{4,1},{5,4},{8,5},{9,8},{12,9},{13,12},{16,13},{17,16},{20,1... | collective-permute-start | bytes 786440 | tf_op jit(solution)/shard_map/ppermute | solution.py:15
  589.0 16.7 %copy-start = (f32[4,2,128,16,128]{2,4,3,1,0:T(8,128)}, f32[4,2,128,16,128]{2,4,3,1,0:T(8,128)S(1)}, u32[]{:S(2)}) copy-start(f32[4,2,128,16,128]{2,4,3,1,0:T(8,128)S(1)} %get-tuple-element.12) | copy-start | bytes 25165828
  589.1 16.6 %copy-start.3 = (f32[4,2,128,16,128]{2,4,3,1,0:T(8,128)}, f32[4,2,128,16,128]{2,4,3,1,0:T(8,128)S(1)}, u32[]{:S(2)}) copy-start(f32[4,2,128,16,128]{2,4,3,1,0:T(8,128)S(1)} %get-tuple-element.11) | copy-start | bytes 25165828
  601.1 10.0 %copy-start.4 = (f32[2,2,128,16,128]{2,4,3,1,0:T(8,128)}, f32[2,2,128,16,128]{2,4,3,1,0:T(8,128)S(1)}, u32[]{:S(2)}) copy-start(f32[2,2,128,16,128]{2,4,3,1,0:T(8,128)S(1)} %get-tuple-element.13) | copy-start | bytes 12582916
  601.1 10.0 %copy-start.5 = (f32[2,2,128,16,128]{2,4,3,1,0:T(8,128)}, f32[2,2,128,16,128]{2,4,3,1,0:T(8,128)S(1)}, u32[]{:S(2)}) copy-start(f32[2,2,128,16,128]{2,4,3,1,0:T(8,128)S(1)} %get-tuple-element.14) | copy-start | bytes 12582916
  601.2 13.1 %collective-permute-start.1 = (bf16[4,2,128,2,128]{2,4,3,1,0:T(8,128)(2,1)S(1)}, bf16[4,2,128,2,128]{2,4,3,1,0:T(8,128)(2,1)S(1)}, u32[]{:S(2)}, u32[]{:S(2)}) collective-permute-start(bf16[4,2,128,2,128]{2,4,3,1,0:T(8,128)(2,1)S(1)} %fusion.54), channel_id=1, source_target_pairs={{1,0},{4,1},{5,4},{8,5},{9,8},{12,9},{13,12},{16,13},{17,16},{20,1... | collective-permute-start | bytes 1572872 | tf_op jit(solution)/shard_map/ppermute | solution.py:15
  626.5 21.4 %slice-start.4 = ((s8[8388608]{0:T(1024)(128)(4,1)}), s8[4194304]{0:T(1024)(128)(4,1)S(1)}, s32[]{:S(2)}) async-start(s8[8388608]{0:T(1024)(128)(4,1)} %bitcast.226), calls=%async_computation.7 | async-start | bytes 8388608
  634.2 13.6 %slice-start.5 = ((s8[8388608]{0:T(1024)(128)(4,1)}), s8[4194304]{0:T(1024)(128)(4,1)S(1)}, s32[]{:S(2)}) async-start(s8[8388608]{0:T(1024)(128)(4,1)} %bitcast.226), calls=%async_computation.8 | async-start | bytes 8388608
  647.8 18.4 %collective-permute-start.2 = (bf16[4,2,128,2,128]{2,4,3,1,0:T(8,128)(2,1)S(1)}, bf16[4,2,128,2,128]{2,4,3,1,0:T(8,128)(2,1)S(1)}, u32[]{:S(2)}, u32[]{:S(2)}) collective-permute-start(bf16[4,2,128,2,128]{2,4,3,1,0:T(8,128)(2,1)S(1)} %slice.450), channel_id=1, source_target_pairs={{29,0},{0,1},{1,4},{4,5},{5,8},{8,9},{9,12},{12,13},{13,16},{16,17... | collective-permute-start | bytes 1572872 | tf_op jit(solution)/shard_map/ppermute | solution.py:15
  680.7 15.5 %slice-start = ((s8[14680064]{0:T(1024)(128)(4,1)}), s8[4194304]{0:T(1024)(128)(4,1)S(1)}, s32[]{:S(2)}) async-start(s8[14680064]{0:T(1024)(128)(4,1)} %bitcast.224), calls=%async_computation.3 | async-start | bytes 8388608
  680.7 15.5 %slice-start.1 = ((s8[14680064]{0:T(1024)(128)(4,1)}), s8[4194304]{0:T(1024)(128)(4,1)S(1)}, s32[]{:S(2)}) async-start(s8[14680064]{0:T(1024)(128)(4,1)} %bitcast.224), calls=%async_computation.4 | async-start | bytes 8388608
  680.7 15.6 %slice-start.2 = ((s8[14680064]{0:T(1024)(128)(4,1)}), s8[2097152]{0:T(1024)(128)(4,1)S(1)}, s32[]{:S(2)}) async-start(s8[14680064]{0:T(1024)(128)(4,1)} %bitcast.224), calls=%async_computation.5 | async-start | bytes 4194304
  690.6 5.6 slice-start.3
  698.1 3.3 copy-start.10
  701.4 8.5 %collective-permute-start.3 = (bf16[4,2,128,1,128]{2,4,3,1,0:T(8,128)(2,1)S(1)}, bf16[4,2,128,1,128]{2,4,3,1,0:T(8,128)(2,1)S(1)}, u32[]{:S(2)}, u32[]{:S(2)}) collective-permute-start(bf16[4,2,128,1,128]{2,4,3,1,0:T(8,128)(2,1)S(1)} %slice.451), channel_id=1, source_target_pairs={{29,0},{0,1},{1,4},{4,5},{5,8},{8,9},{9,12},{12,13},{13,16},{16,17... | collective-permute-start | bytes 786440 | tf_op jit(solution)/shard_map/ppermute | solution.py:15
  721.4 4.9 copy-start.2
  732.0 3.4 copy-start.9
  (3 other events, 8.3 us)
Sparse Core Ops, SparseCore 0:
  527.2 41.1 all-reduce.1
